TPU v7x, 32 devices: a whole 2x2x4 slice. The times are simulated.
32 devices in a mesh: ia: 4 (over y, x), ja: 4 (over z), col: 2 (over core).
Axes of the slice: x: 2, y: 2, z: 4, core: 2. Of those that a mesh axis runs over, the one named last changes fastest.
Arguments:
- pair_rep: bfloat16 [512, 512, 128], P('ia', 'ja'), may hold values from -6 to 6
- norm_gain: float32 [128], replicated, may hold values from 0.1 to 1.9
- weights: bfloat16 [4, 128, 128], P(None, None, 'col'), may hold values from -0.5 to 0.5
- residue_mask: int32 [512], replicated, may hold values 0 or 1
- product_grad: bfloat16 [512, 128, 512], P('ia', 'col', 'ja'), may hold values from -1 to 1
Outputs:
- pair_grad: bfloat16 [512, 512, 128], P('ia', 'ja')
- weight_grads: float32 [4, 128, 128], P(None, None, 'col')
All inputs are finite; a program needn't handle non-finite values.
Results may differ from a plain program's by a relative error of at most 0.0067.
Values may be sent and summed in bfloat16 or wider, within the bound.
A program may use at most 128 MiB of HBM per device.

v0:
```python
import jax
import jax.numpy as jnp
from jax import lax
from jax.sharding import PartitionSpec as P

CLIP_LIMIT = 64.0


def gate_terms(incoming, linear, gate_pre, pair_valid):
    sigmoid_gate = jax.nn.sigmoid(gate_pre)
    through = incoming * pair_valid
    return (through * sigmoid_gate, through * linear * sigmoid_gate * (1.0 - sigmoid_gate))


def on_device(pair_rep, norm_gain, weights, residue_mask, product_grad):
    row_count = pair_rep.shape[0]
    col_count = pair_rep.shape[1]
    row_first = lax.axis_index("ia") * row_count
    col_first = lax.axis_index("ja") * col_count
    validity = residue_mask.astype(jnp.float32)
    row_valid = lax.dynamic_slice_in_dim(validity, row_first, row_count)
    col_valid = lax.dynamic_slice_in_dim(validity, col_first, col_count)
    pair_valid = row_valid[:, None, None] * col_valid[None, None, :]
    floats = pair_rep.astype(jnp.float32)
    centred = floats - jnp.mean(floats, axis=-1, keepdims=True)
    inv_std = lax.rsqrt(jnp.mean(centred * centred, axis=-1, keepdims=True) + 1e-05)
    unit_rows = centred * inv_std
    normed = (unit_rows * norm_gain).astype(jnp.bfloat16)
    projected = jnp.einsum("ikd,wdc->wick", normed, weights, preferred_element_type=jnp.float32)
    left_side = (pair_valid * jax.nn.sigmoid(projected[1]) * projected[0]).astype(jnp.bfloat16)
    right_side = (pair_valid * jax.nn.sigmoid(projected[3]) * projected[2]).astype(jnp.bfloat16)
    row_panel = lax.all_gather(product_grad, "ja", axis=2, tiled=True)
    panel_part = row_panel
    grad_left = jnp.einsum(
        "icj,jck->ick",
        panel_part,
        lax.all_gather(right_side, "ia", axis=0, tiled=True),
        preferred_element_type=jnp.float32,
    )
    panel_part = row_panel
    grad_right = lax.psum_scatter(
        jnp.einsum("icj,ick->jck", panel_part, left_side, preferred_element_type=jnp.float32),
        "ia",
        scatter_dimension=0,
        tiled=True,
    )
    lin_a, gate_a = gate_terms(grad_left, projected[0], projected[1], pair_valid)
    lin_b, gate_b = gate_terms(grad_right, projected[2], projected[3], pair_valid)
    proj_grads = jnp.stack([lin_a, gate_a, lin_b, gate_b]).astype(jnp.bfloat16)
    grad_part = jnp.einsum("ikd,wick->wdc", normed, proj_grads, preferred_element_type=jnp.float32)
    input_part = jnp.einsum(
        "wick,wdc->ikd", proj_grads, weights, preferred_element_type=jnp.float32
    )
    normed_grad = lax.psum(input_part, "col")
    scaled = normed_grad * norm_gain
    pair_grad = inv_std * (
        scaled
        - jnp.mean(scaled, axis=-1, keepdims=True)
        - unit_rows * jnp.mean(scaled * unit_rows, axis=-1, keepdims=True)
    )
    summed = lax.psum(grad_part, ("ia", "ja"))
    squares = lax.psum(jnp.sum(summed * summed), "col")
    factor = jnp.minimum(1.0, CLIP_LIMIT * lax.rsqrt(squares + 1e-06))
    weight_grads = summed * factor
    return (pair_grad.astype(jnp.bfloat16), weight_grads)


def solution(mesh):
    placed = (P("ia", "ja", None), P(), P(None, None, "col"), P(), P("ia", "col", "ja"))
    return jax.shard_map(
        on_device,
        mesh=mesh,
        in_specs=placed,
        out_specs=(P("ia", "ja", None), P(None, None, "col")),
        check_vma=False,
    )
```

profile of v0, /device:TPU:0, one launch (start us, length us, event | category | flops | bytes accessed | tf_op | source)
XLA Modules:
  0.0 660.3 jit_solution(14896707460684824877)
XLA Ops:
  7.2 4.3 copy.18
  11.8 3.5 convert_reduce_fusion
  15.3 4.8 fusion.10
  20.2 4.7 convolution_bitcast_fusion
  24.9 5.9 copy-done.1
  30.8 2.6 multiply_convert_fusion.5
  33.9 129.6 %all-gather.5.cloned.1.call-done = bf16[128,64,512]{2,0,1:T(8,128)(2,1)} async-done(((bf16[128,64,128]{2,0,1:T(8,128)(2,1)}), bf16[128,64,512]{2,0,1:T(8,128)(2,1)}) %all-gather.5.cloned.1.call-update) | async-done | bytes 8388624 | tf_op jit(solution)/shard_map/all_gather | solution.py:32
  163.5 87.5 %all-gather.3.cloned.1.call-done = bf16[512,64,128]{2,1,0:T(8,128)(2,1)} async-done(((bf16[128,64,128]{2,1,0:T(8,128)(2,1)}), bf16[512,64,128]{2,1,0:T(8,128)(2,1)}) %all-gather.3.cloned.1.call-update) | async-done | bytes 8388624 | tf_op jit(solution)/shard_map/all_gather | solution.py:37
  251.0 25.2 %fusion.11 = f32[64,128,128]{2,1,0:T(8,128)} fusion(bf16[128,64,512]{2,0,1:T(8,128)(2,1)} %all-gather.5.cloned.1.call-done, bf16[512,64,128]{2,1,0:T(8,128)(2,1)} %all-gather.3.cloned.1.call-done), kind=kOutput, calls=%fused_computation.15 | convolution fusion | flops 1073741824 | bytes 20971520 | tf_op jit(solution)/shard_map/icj,jck->ick/dot_general | solution.py:34
  276.2 5.4 copy.20
  281.6 6.8 %fusion.28 = (bf16[1,128,64,128]{3,2,1,0:T(8,128)(2,1)S(1)}, bf16[1,128,64,128]{3,2,1,0:T(8,128)(2,1)}, bf16[128,64,128]{2,1,0:T(8,128)(2,1)S(1)}) fusion(f32[64,128,128]{1,0,2:T(8,128)} %copy.20, f32[128,128]{1,0:T(8,128)S(1)} %broadcast_multiply_fusion.1, f32[4,128,64,128]{3,2,0,1:T(8,128)} %copy-done.1), kind=kLoop, calls=%fused_computation.43 | loop fusion | flops 14680064 | bytes 18939904 | tf_op jit(solution)/shard_map/stack | solution.py:49
  288.5 14.1 %fusion.32 = f32[64,128,512]{2,1,0:T(8,128)} fusion(bf16[128,64,512]{2,0,1:T(8,128)(2,1)} %all-gather.5.cloned.1.call-done, bf16[128,64,128]{2,1,0:T(8,128)(2,1)S(1)} %get-tuple-element.8), kind=kOutput, calls=%fused_computation.47 | convolution fusion | flops 1073741824 | bytes 27262976 | tf_op jit(solution)/shard_map/icj,ick->jck/dot_general | solution.py:42
  302.6 16.6 %copy.23 = f32[64,128,512]{1,0,2:T(8,128)} copy(f32[64,128,512]{2,1,0:T(8,128)} %fusion.32) | data formatting | bytes 33554432 | tf_op jit(solution)/shard_map/icj,ick->jck/dot_general | solution.py:42
  319.2 153.8 %reduce-scatter.2.cloned.1.call-done = f32[128,64,128]{2,1,0:T(8,128)} async-done(((f32[512,64,128]{2,1,0:T(8,128)}), f32[128,64,128]{2,1,0:T(8,128)}) %reduce-scatter.2.cloned.1.call-update) | async-done | bytes 4194320 | tf_op jit(solution)/shard_map/reduce_scatter | solution.py:41
  473.1 6.0 fusion.30
  481.1 5.4 fusion.34
  486.6 6.5 convolution_bitcast_fusion.1
  493.1 99.0 %all-reduce.5.cloned.1.call-done = f32[4,128,64]{1,2,0:T(8,128)} async-done(((f32[4,128,64]{1,2,0:T(8,128)}), f32[4,128,64]{1,2,0:T(8,128)}) %all-reduce.5.cloned.1.call-update) | async-done | bytes 131088 | tf_op jit(solution)/shard_map/psum | solution.py:61
  592.1 1.5 multiply_reduce_fusion.1
  593.7 3.1 psum.23
  597.4 1.6 broadcast_multiply_fusion
  599.0 32.2 %all-reduce.3.cloned.1.call-done = f32[128,128,128]{2,1,0:T(8,128)} async-done(((f32[128,128,128]{2,1,0:T(8,128)}), f32[128,128,128]{2,1,0:T(8,128)}) %all-reduce.3.cloned.1.call-update) | async-done | bytes 8388624 | tf_op jit(solution)/shard_map/psum | solution.py:54
  631.2 11.6 %multiply_reduce_fusion = (f32[128,128]{1,0:T(8,128)S(1)}, f32[128,128]{1,0:T(8,128)S(1)}) fusion(f32[128,128,128]{2,1,0:T(8,128)} %all-reduce.3.cloned.1.call-done, f32[128]{0:T(128)S(1)} %copy-done.9, f32[128,128]{1,0:T(8,128)S(1)} %add_rsqrt_fusion, f32[128,128]{1,0:T(8,128)S(1)} %broadcast_multiply_fusion.4, bf16[128,128,128]{2,1,0:T(8,128)(2,1)} %param.5), kind=kLoop, calls=%fused_computation.17 | loop fusion | flops 14647296 | bytes 12845568 | tf_op jit(solution)/shard_map/reduce_sum | solution.py:58
  642.8 10.7 %fusion.9 = bf16[128,128,128]{2,1,0:T(8,128)(2,1)} fusion(bf16[128,128,128]{2,1,0:T(8,128)(2,1)S(1)} %copy-done.4, f32[128,128,128]{2,1,0:T(8,128)S(1)} %copy-done.5, f32[128,128]{1,0:T(8,128)S(1)} %get-tuple-element.11, f32[128,128]{1,0:T(8,128)S(1)} %get-tuple-element.12, f32[128]{0:T(128)S(1)} %copy-done.9, f32[128,128]{1,0:T(8,128)S(1)} %add_rsqrt_fusion, ...), kind=kLoop, calls=%fused_computation.12 | loop fusion | flops 18874368 | bytes 17039872 | tf_op jit(solution)/shard_map/convert_element_type | solution.py:65
  (37 shorter events, 3.0 us)
Async XLA Ops:
  7.2 13.0 %copy-start = (bf16[4,128,64]{1,2,0:T(8,128)(2,1)S(1)}, bf16[4,128,64]{1,2,0:T(8,128)(2,1)}, u32[]{:S(2)}) copy-start(bf16[4,128,64]{1,2,0:T(8,128)(2,1)} %param.7) | copy-start | bytes 196612
  7.2 4.4 copy-start.10
  7.2 156.3 %all-gather.5.cloned.1.call-start = ((), (), s32[]{:S(2)}) async-start(), calls=%async_computation.2 | async-start | bytes 10485760 | tf_op jit(solution)/shard_map/all_gather | solution.py:32
  11.5 239.5 %all-gather.3.cloned.1.call-start = ((), (), s32[]{:S(2)}) async-start(), calls=%async_computation.1 | async-start | bytes 10485760 | tf_op jit(solution)/shard_map/all_gather | solution.py:37
  11.6 3.7 copy-start.2
  11.8 8.4 %copy-start.9 = (f32[128]{0:T(128)S(1)}, f32[128]{0:T(128)}, u32[]{:S(2)}) copy-start(f32[128]{0:T(128)} %param.6) | copy-start | bytes 1540
  24.9 5.9 copy-start.1
  33.4 439.6 %reduce-scatter.2.cloned.1.call-start = ((), (), s32[]{:S(2)}) async-start(), calls=%async_computation.3 | async-start | bytes 20971520 | tf_op jit(solution)/shard_map/reduce_scatter | solution.py:41
  319.2 272.9 %all-reduce.5.cloned.1.call-start = ((), (), s32[]{:S(2)}) async-start(), calls=%async_computation.5 | async-start | bytes 262144 | tf_op jit(solution)/shard_map/psum | solution.py:61
  473.1 8.0 %copy-start.3 = (bf16[128,128,128]{2,1,0:T(8,128)(2,1)S(1)}, bf16[128,128,128]{2,1,0:T(8,128)(2,1)}, u32[]{:S(2)}) copy-start(bf16[128,128,128]{2,1,0:T(8,128)(2,1)} %param.5) | copy-start | bytes 12582916
  473.1 8.0 %copy-start.6 = (bf16[1,128,64,128]{3,2,1,0:T(8,128)(2,1)S(1)}, bf16[1,128,64,128]{3,2,1,0:T(8,128)(2,1)}, u32[]{:S(2)}) copy-start(bf16[1,128,64,128]{3,2,1,0:T(8,128)(2,1)} %get-tuple-element.5) | copy-start | bytes 6291460
  479.1 1.3 copy-start.7
  479.1 2.0 copy-start.8
  486.6 144.6 %all-reduce.3.cloned.1.call-start = ((), (), s32[]{:S(2)}) async-start(), calls=%async_computation.4 | async-start | bytes 16777216 | tf_op jit(solution)/shard_map/psum | solution.py:54
  631.2 11.6 %copy-start.4 = (bf16[128,128,128]{2,1,0:T(8,128)(2,1)S(1)}, bf16[128,128,128]{2,1,0:T(8,128)(2,1)}, u32[]{:S(2)}) copy-start(bf16[128,128,128]{2,1,0:T(8,128)(2,1)} %param.5) | copy-start | bytes 12582916
  631.2 11.6 %copy-start.5 = (f32[128,128,128]{2,1,0:T(8,128)S(1)}, f32[128,128,128]{2,1,0:T(8,128)}, u32[]{:S(2)}) copy-start(f32[128,128,128]{2,1,0:T(8,128)} %all-reduce.3.cloned.1.call-done) | copy-start | bytes 25165828
Sparse Core Ops, SparseCore 0:
  11.6 151.8 all-gather.4
  165.4 85.6 all-gather.2
  319.3 153.7 reduce-scatter.1
  486.7 105.3 all-reduce.4
  594.4 36.6 all-reduce.2
where the time goes:
time: 668 us; the launch traced here: 660 us
  waiting for transfers between devices  502 us (75%)
  matrix products  55.9 us (8%)
  other arithmetic  49.3 us (7%)
  local copies, waits for them, and re-layouts  34.2 us (5%)
  between operations  14.9 us (2%)
    reduce_scatter x1, waiting for transfers between devices, on_device(): lax.psum_scatter(jnp.einsum('icj,ick->jck', panel_part, left_side, prefer...  154 us
    all_gather x1, waiting for transfers between devices, on_device(): row_panel = lax.all_gather(product_grad, 'ja', axis=2, tiled=True)  130 us
    psum x1, waiting for transfers between devices, on_device(): summed = lax.psum(grad_part, ('ia', 'ja'))  99 us
    all_gather x1, waiting for transfers between devices, on_device(): lax.all_gather(right_side, 'ia', axis=0, tiled=True)  87.5 us
    psum x1, waiting for transfers between devices, on_device(): normed_grad = lax.psum(input_part, 'col')  32.2 us
    dot_general x1, matrix products, on_device(): jnp.einsum('icj,jck->ick', panel_part, lax.all_gather(right_side, 'ia', a...  25.2 us
    dot_general x1, local copies, waits for them, and re-layouts, on_device(): jnp.einsum('icj,ick->jck', panel_part, left_side, preferred_element_type=...  16.6 us
    dot_general x1, matrix products, on_device(): jnp.einsum('icj,ick->jck', panel_part, left_side, preferred_element_type=...  14.1 us
  transfers between devices with their start and end apart: 5, of which 5 were waited for; matrix products, arithmetic and copies ran while one was open for 4% of the time, Pallas kernels for 0%

commit v1 on v0

--- a/solution.py
+++ b/solution.py
@@ -31,12 +31,37 @@
     right_side = (pair_valid * jax.nn.sigmoid(projected[3]) * projected[2]).astype(jnp.bfloat16)
     row_panel = lax.all_gather(product_grad, "ja", axis=2, tiled=True)
     panel_part = row_panel
+    value_now, p_next, y = (lax.axis_size("ia"), lax.axis_index("ia"), right_side.shape[0])
+    trail = [(s, (s + 1) % value_now) for s in range(value_now)]
+    local_next = value_now // 2
+    spare = block_next = right_side
     grad_left = jnp.einsum(
         "icj,jck->ick",
-        panel_part,
-        lax.all_gather(right_side, "ia", axis=0, tiled=True),
+        lax.dynamic_slice_in_dim(panel_part, p_next * y, right_side.shape[0], axis=2),
+        right_side,
         preferred_element_type=jnp.float32,
     )
+    pile = [(s, (s - 1) % value_now) for s in range(value_now)]
+    for hop_no in range(1, local_next + 1):
+        spare = lax.ppermute(spare, perm=trail, axis_name="ia")
+        if hop_no < value_now - local_next:
+            block_next = lax.ppermute(block_next, perm=pile, axis_name="ia")
+            grad_left = grad_left + jnp.einsum(
+                "icj,jck->ick",
+                lax.dynamic_slice_in_dim(
+                    panel_part, (p_next + hop_no) % value_now * y, block_next.shape[0], axis=2
+                ),
+                block_next,
+                preferred_element_type=jnp.float32,
+            )
+        grad_left = grad_left + jnp.einsum(
+            "icj,jck->ick",
+            lax.dynamic_slice_in_dim(
+                panel_part, (p_next - hop_no) % value_now * y, spare.shape[0], axis=2
+            ),
+            spare,
+            preferred_element_type=jnp.float32,
+        )
     panel_part = row_panel
     grad_right = lax.psum_scatter(
         jnp.einsum("icj,ick->jck", panel_part, left_side, preferred_element_type=jnp.float32),

time: 668 us -> 606 us (0.907)
  waiting for transfers between devices: 502 us -> 409 us
  local copies, waits for them, and re-layouts: 34.2 us -> 51.1 us
  other arithmetic: 49.3 us -> 57.8 us
    all_gather x1, waiting for transfers between devices: 130 us -> 32 us  [on_device(): row_panel = lax.all_gather(product_grad, 'ja', axis=2, tiled=True)]
    ppermute x0 -> x3, waiting for transfers between devices: none -> 93 us  [the longest x2 93 us: on_device(): spare = lax.ppermute(spare, perm=trail, axis_name='ia')]
    all_gather x1 -> x0, waiting for transfers between devices: 87.5 us -> none  [on_device(): lax.all_gather(right_side, 'ia', axis=0, tiled=True)]
    dot_general x1 -> x4, local copies, waits for them, and re-layouts: 5.42 us -> 21.6 us  [the longest x2 10.8 us: on_device(): jnp.einsum('icj,jck->ick', lax.dynamic_slice_in_dim(panel_part, (p_next -...]
    another operation x2, other arithmetic: 12.9 us -> 22.7 us  [on_device(): proj_grads = jnp.stack([lin_a, gate_a, lin_b, gate_b]).astype(jnp.bfloat16)]
    dot_general x1 -> x4, matrix products: 25.2 us -> 24.7 us  [the longest x2 12.6 us: on_device(): jnp.einsum('icj,jck->ick', lax.dynamic_slice_in_dim(panel_part, (p_next -...]
  transfers between devices with their start and end apart: 5 -> 7, of which waited for: 5 -> 6; matrix products, arithmetic and copies ran while one was open for 4% -> 6% of each run, Pallas kernels for 0% -> 0%
where the time goes in v1:
time: 606 us; the launch traced here: 598 us
  waiting for transfers between devices  409 us (67%)
  other arithmetic  57.8 us (10%)
  matrix products  55.6 us (9%)
  local copies, waits for them, and re-layouts  51.1 us (8%)
  between operations  14.9 us (2%)
  starting transfers between devices  6.55 us (1%)
    reduce_scatter x1, waiting for transfers between devices, on_device(): lax.psum_scatter(jnp.einsum('icj,ick->jck', panel_part, left_side, prefer...  153 us
    psum x1, waiting for transfers between devices, on_device(): summed = lax.psum(grad_part, ('ia', 'ja'))  98.8 us
    ppermute x2, waiting for transfers between devices, on_device(): spare = lax.ppermute(spare, perm=trail, axis_name='ia')  93 us
    psum x1, waiting for transfers between devices, on_device(): normed_grad = lax.psum(input_part, 'col')  32.2 us
    all_gather x1, waiting for transfers between devices, on_device(): row_panel = lax.all_gather(product_grad, 'ja', axis=2, tiled=True)  32 us
    another operation x2, other arithmetic, on_device(): proj_grads = jnp.stack([lin_a, gate_a, lin_b, gate_b]).astype(jnp.bfloat16)  22.7 us
    dot_general x1, local copies, waits for them, and re-layouts, on_device(): jnp.einsum('icj,ick->jck', panel_part, left_side, preferred_element_type=...  16.6 us
    dot_general x1, matrix products, on_device(): jnp.einsum('icj,ick->jck', panel_part, left_side, preferred_element_type=...  14.1 us
  transfers between devices with their start and end apart: 7, of which 6 were waited for; matrix products, arithmetic and copies ran while one was open for 6% of the time, Pallas kernels for 0%

profile of v1, /device:TPU:0, one launch (start us, length us, event | category | flops | bytes accessed | tf_op | source)
XLA Modules:
  0.0 597.8 jit_solution(7024431213077011554)
XLA Ops:
  15.3 4.8 fusion.10
  24.9 5.9 copy-done.1
  35.1 46.7 %collective-permute-done.1 = bf16[128,64,128]{2,1,0:T(8,128)(2,1)} collective-permute-done((bf16[128,64,128]{2,1,0:T(8,128)(2,1)S(1)}, bf16[128,64,128]{2,1,0:T(8,128)(2,1)}, u32[]{:S(2)}, u32[]{:S(2)}) %collective-permute-start.1) | collective-permute-done | bytes 2097184 | tf_op jit(solution)/shard_map/ppermute | solution.py:46
  85.1 46.3 %collective-permute-done.2 = bf16[128,64,128]{2,1,0:T(8,128)(2,1)} collective-permute-done((bf16[128,64,128]{2,1,0:T(8,128)(2,1)}, bf16[128,64,128]{2,1,0:T(8,128)(2,1)}, u32[]{:S(2)}, u32[]{:S(2)}) %collective-permute-start.2) | collective-permute-done | bytes 2097184 | tf_op jit(solution)/shard_map/ppermute | solution.py:46
  131.5 32.0 %all-gather.2.cloned.1.call-done = bf16[128,64,512]{2,0,1:T(8,128)(2,1)} async-done(((bf16[128,64,128]{2,0,1:T(8,128)(2,1)}), bf16[128,64,512]{2,0,1:T(8,128)(2,1)}) %all-gather.2.cloned.1.call-update) | async-done | bytes 8388624 | tf_op jit(solution)/shard_map/all_gather | solution.py:32
  163.5 6.3 %fusion.32 = f32[64,128,128]{2,1,0:T(8,128)} fusion(bf16[128,64,128]{2,1,0:T(8,128)(2,1)} %collective-permute-done.2, bf16[128,64,512]{2,0,1:T(8,128)(2,1)} %all-gather.2.cloned.1.call-done, s32[]{:T(128)S(6)} %select_n.38), kind=kOutput, calls=%fused_computation.47 | convolution fusion | flops 268435456 | bytes 8388612 | tf_op jit(solution)/shard_map/icj,jck->ick/dot_general | solution.py:57
  169.8 5.4 copy.17
  175.3 6.3 %fusion.36 = f32[64,128,128]{2,1,0:T(8,128)} fusion(bf16[128,64,128]{2,1,0:T(8,128)(2,1)} %collective-permute-done, bf16[128,64,512]{2,0,1:T(8,128)(2,1)} %all-gather.2.cloned.1.call-done, s32[]{:T(128)S(6)} %select_n.34), kind=kOutput, calls=%fused_computation.51 | convolution fusion | flops 268435456 | bytes 8388612 | tf_op jit(solution)/shard_map/icj,jck->ick/dot_general | solution.py:49
  181.6 5.4 copy.13
  187.0 6.3 %fusion.34 = f32[64,128,128]{2,1,0:T(8,128)} fusion(bf16[128,64,128]{2,1,0:T(8,128)(2,1)} %collective-permute-done.1, bf16[128,64,512]{2,0,1:T(8,128)(2,1)} %all-gather.2.cloned.1.call-done, s32[]{:T(128)S(6)} %select_n.36), kind=kOutput, calls=%fused_computation.49 | convolution fusion | flops 268435456 | bytes 8388612 | tf_op jit(solution)/shard_map/icj,jck->ick/dot_general | solution.py:57
  193.3 5.4 copy.15
  198.7 5.7 fusion.38
  204.4 5.4 copy.12
  209.8 12.3 %fusion.26 = (bf16[1,128,64,128]{3,2,1,0:T(8,128)(2,1)S(1)}, f32[128,64,128]{2,1,0:T(8,128)}, bf16[128,64,128]{2,1,0:T(8,128)(2,1)S(1)}) fusion(f32[4,128,64,128]{3,2,0,1:T(8,128)} %copy-done.1, f32[128,128]{1,0:T(8,128)S(1)} %broadcast_multiply_fusion.1, f32[64,128,128]{1,0,2:T(8,128)} %copy.17, f32[64,128,128]{1,0,2:T(8,128)} %copy.15, ...), kind=kLoop, calls=%fused_computation.41 | loop fusion | flops 12582912 | bytes 33619968 | tf_op jit(solution)/shard_map/stack | solution.py:74
  222.1 14.1 %fusion.30 = f32[64,128,512]{2,1,0:T(8,128)} fusion(bf16[128,64,512]{2,0,1:T(8,128)(2,1)} %all-gather.2.cloned.1.call-done, bf16[128,64,128]{2,1,0:T(8,128)(2,1)S(1)} %get-tuple-element.8), kind=kOutput, calls=%fused_computation.45 | convolution fusion | flops 1073741824 | bytes 27262976 | tf_op jit(solution)/shard_map/icj,ick->jck/dot_general | solution.py:67
  236.3 16.6 %copy.20 = f32[64,128,512]{1,0,2:T(8,128)} copy(f32[64,128,512]{2,1,0:T(8,128)} %fusion.30) | data formatting | bytes 33554432 | tf_op jit(solution)/shard_map/icj,ick->jck/dot_general | solution.py:67
  252.9 152.7 %reduce-scatter.2.cloned.1.call-done = f32[128,64,128]{2,1,0:T(8,128)} async-done(((f32[512,64,128]{2,1,0:T(8,128)}), f32[128,64,128]{2,1,0:T(8,128)}) %reduce-scatter.2.cloned.1.call-update) | async-done | bytes 4194320 | tf_op jit(solution)/shard_map/reduce_scatter | solution.py:66
  405.6 10.3 %fusion.28 = (bf16[1,128,64,128]{3,2,1,0:T(8,128)(2,1)S(1)}, bf16[1,128,64,128]{3,2,1,0:T(8,128)(2,1)S(1)}, bf16[1,128,64,128]{3,2,1,0:T(8,128)(2,1)S(1)}) fusion(f32[128,64,128]{2,1,0:T(8,128)} %reduce-scatter.2.cloned.1.call-done, f32[128,128]{1,0:T(8,128)S(1)} %broadcast_multiply_fusion.1, f32[4,128,64,128]{3,2,0,1:T(8,128)} %copy-done.1, ...), kind=kLoop, calls=%fused_computation.43 | loop fusion | flops 19922944 | bytes 31522816 | tf_op jit(solution)/shard_map/stack | solution.py:74
  418.6 5.4 fusion.44
  424.1 6.7 %convolution_bitcast_fusion.1 = f32[128,128,128]{2,1,0:T(8,128)} fusion(bf16[1,128,64,128]{3,2,1,0:T(8,128)(2,1)} %copy-done.7, bf16[1,128,64,128]{3,2,1,0:T(8,128)(2,1)} %copy-done.6, bf16[1,128,64,128]{3,2,1,0:T(8,128)(2,1)} %copy-done.8, bf16[1,128,64,128]{3,2,1,0:T(8,128)(2,1)S(1)} %get-tuple-element.4, bf16[4,128,64]{1,2,0:T(8,128)(2,1)S(1)} %copy-done), kind=kOutput, calls=%fused_computation.40 | convolution fusion | flops 1086324736 | bytes 16842752 | tf_op jit(solution)/shard_map/wick,wdc->ikd/dot_general | solution.py:76
  430.8 98.8 %all-reduce.5.cloned.1.call-done = f32[4,128,64]{1,2,0:T(8,128)} async-done(((f32[4,128,64]{1,2,0:T(8,128)}), f32[4,128,64]{1,2,0:T(8,128)}) %all-reduce.5.cloned.1.call-update) | async-done | bytes 131088 | tf_op jit(solution)/shard_map/psum | solution.py:86
  536.5 32.2 %all-reduce.3.cloned.1.call-done = f32[128,128,128]{2,1,0:T(8,128)} async-done(((f32[128,128,128]{2,1,0:T(8,128)}), f32[128,128,128]{2,1,0:T(8,128)}) %all-reduce.3.cloned.1.call-update) | async-done | bytes 8388624 | tf_op jit(solution)/shard_map/psum | solution.py:79
  568.6 11.6 %multiply_reduce_fusion = (f32[128,128]{1,0:T(8,128)S(1)}, f32[128,128]{1,0:T(8,128)S(1)}) fusion(f32[128,128,128]{2,1,0:T(8,128)} %all-reduce.3.cloned.1.call-done, f32[128]{0:T(128)S(1)} %copy-done.9, f32[128,128]{1,0:T(8,128)S(1)} %add_rsqrt_fusion, f32[128,128]{1,0:T(8,128)S(1)} %broadcast_multiply_fusion.4, bf16[128,128,128]{2,1,0:T(8,128)(2,1)} %param.5), kind=kLoop, calls=%fused_computation.15 | loop fusion | flops 14647296 | bytes 12845568 | tf_op jit(solution)/shard_map/reduce_sum | solution.py:83
  580.3 10.7 %fusion.9 = bf16[128,128,128]{2,1,0:T(8,128)(2,1)} fusion(bf16[128,128,128]{2,1,0:T(8,128)(2,1)S(1)} %copy-done.4, f32[128,128,128]{2,1,0:T(8,128)S(1)} %copy-done.5, f32[128,128]{1,0:T(8,128)S(1)} %get-tuple-element.12, f32[128,128]{1,0:T(8,128)S(1)} %get-tuple-element.13, f32[128]{0:T(128)S(1)} %copy-done.9, f32[128,128]{1,0:T(8,128)S(1)} %add_rsqrt_fusion, ...), kind=kLoop, calls=%fused_computation.12 | loop fusion | flops 18874368 | bytes 17039872 | tf_op jit(solution)/shard_map/convert_element_type | solution.py:90
  (46 shorter events, 29.5 us)
Async XLA Ops:
  7.2 13.0 %copy-start = (bf16[4,128,64]{1,2,0:T(8,128)(2,1)S(1)}, bf16[4,128,64]{1,2,0:T(8,128)(2,1)}, u32[]{:S(2)}) copy-start(bf16[4,128,64]{1,2,0:T(8,128)(2,1)} %param.7) | copy-start | bytes 196612
  7.2 4.4 copy-start.10
  7.2 156.3 %all-gather.2.cloned.1.call-start = ((), (), s32[]{:S(2)}) async-start(), calls=%async_computation.1 | async-start | bytes 10485760 | tf_op jit(solution)/shard_map/all_gather | solution.py:32
  11.5 394.0 %reduce-scatter.2.cloned.1.call-start = ((), (), s32[]{:S(2)}) async-start(), calls=%async_computation.2 | async-start | bytes 20971520 | tf_op jit(solution)/shard_map/reduce_scatter | solution.py:66
  11.6 3.7 copy-start.2
  11.8 8.4 %copy-start.9 = (f32[128]{0:T(128)S(1)}, f32[128]{0:T(128)}, u32[]{:S(2)}) copy-start(f32[128]{0:T(128)} %param.6) | copy-start | bytes 1540
  24.9 5.9 copy-start.1
  32.1 49.7 %collective-permute-start.1 = (bf16[128,64,128]{2,1,0:T(8,128)(2,1)S(1)}, bf16[128,64,128]{2,1,0:T(8,128)(2,1)}, u32[]{:S(2)}, u32[]{:S(2)}) collective-permute-start(bf16[128,64,128]{2,1,0:T(8,128)(2,1)S(1)} %multiply_convert_fusion.5), channel_id=1, source_target_pairs={{0,8},{8,16},{16,24},{24,0},{1,9},{9,17},{17,25},{25,1},{2,10},{10... | collective-permute-start | bytes 6291464 | tf_op jit(solution)/shard_map/ppermute | solution.py:46
  81.8 49.7 %collective-permute-start.2 = (bf16[128,64,128]{2,1,0:T(8,128)(2,1)}, bf16[128,64,128]{2,1,0:T(8,128)(2,1)}, u32[]{:S(2)}, u32[]{:S(2)}) collective-permute-start(bf16[128,64,128]{2,1,0:T(8,128)(2,1)} %collective-permute-done.1), channel_id=1, source_target_pairs={{0,8},{8,16},{16,24},{24,0},{1,9},{9,17},{17,25},{25,1},{2,10},{10... | collective-permute-start | bytes 6291464 | tf_op jit(solution)/shard_map/ppermute | solution.py:46
  82.6 92.7 %collective-permute-start = (bf16[128,64,128]{2,1,0:T(8,128)(2,1)S(1)}, bf16[128,64,128]{2,1,0:T(8,128)(2,1)}, u32[]{:S(2)}, u32[]{:S(2)}) collective-permute-start(bf16[128,64,128]{2,1,0:T(8,128)(2,1)S(1)} %multiply_convert_fusion.5), channel_id=1, source_target_pairs={{0,24},{8,0},{16,8},{24,16},{1,25},{9,1},{17,9},{25,17},{2,26},{10... | collective-permute-start | bytes 6291464 | tf_op jit(solution)/shard_map/ppermute | solution.py:48
  252.8 276.7 %all-reduce.5.cloned.1.call-start = ((), (), s32[]{:S(2)}) async-start(), calls=%async_computation.4 | async-start | bytes 262144 | tf_op jit(solution)/shard_map/psum | solution.py:86
  405.5 13.0 %copy-start.3 = (bf16[128,128,128]{2,1,0:T(8,128)(2,1)S(1)}, bf16[128,128,128]{2,1,0:T(8,128)(2,1)}, u32[]{:S(2)}) copy-start(bf16[128,128,128]{2,1,0:T(8,128)(2,1)} %param.5) | copy-start | bytes 12582916
  415.9 1.4 copy-start.6
  415.9 2.0 copy-start.7
  415.9 2.7 copy-start.8
  424.0 144.6 %all-reduce.3.cloned.1.call-start = ((), (), s32[]{:S(2)}) async-start(), calls=%async_computation.3 | async-start | bytes 16777216 | tf_op jit(solution)/shard_map/psum | solution.py:79
  568.6 11.6 %copy-start.4 = (bf16[128,128,128]{2,1,0:T(8,128)(2,1)S(1)}, bf16[128,128,128]{2,1,0:T(8,128)(2,1)}, u32[]{:S(2)}) copy-start(bf16[128,128,128]{2,1,0:T(8,128)(2,1)} %param.5) | copy-start | bytes 12582916
  568.6 11.6 %copy-start.5 = (f32[128,128,128]{2,1,0:T(8,128)S(1)}, f32[128,128,128]{2,1,0:T(8,128)}, u32[]{:S(2)}) copy-start(f32[128,128,128]{2,1,0:T(8,128)} %all-reduce.3.cloned.1.call-done) | copy-start | bytes 25165828
Sparse Core Ops, SparseCore 0:
  11.6 151.8 all-gather.1
  253.0 152.5 reduce-scatter.1
  424.2 105.3 all-reduce.4
  531.9 36.6 all-reduce.2
